TPU v7x, 32 devices: a whole 2x2x4 slice. The times are simulated.
32 devices in a mesh: row: 8 (over z, x), col: 4 (over y, core).
Axes of the slice: x: 2, y: 2, z: 4, core: 2. Of those that a mesh axis runs over, the one named last changes fastest.
Arguments:
- density_first: bfloat16 [12288, 12288], P('row', 'col'), may hold values from -0.0068359375 to 0.0068359375
- density_second: bfloat16 [12288, 12288], P('row', 'col'), may hold values from -0.0068359375 to 0.0068359375
- basis: bfloat16 [64, 4096, 896], P(('row', 'col')), may hold values from -6 to 6
- tile_list: int32 [64, 7], P(('row', 'col')), may hold values from 0 to 95, as said below
- tile_count: int32 [64], P(('row', 'col')), may hold values from 5 to 7, as said below
- point_count: int32 [64], P(('row', 'col')), may hold values from 1024 to 4096, as said below
- offsets: float32 [3, 64, 4096], P(None, ('row', 'col')), may hold values from -5 to 5
- weights: float32 [64, 4096], P(('row', 'col')), may hold values from 0.05 to 1
- atom_of_point: int32 [64, 4096], P(('row', 'col')), may hold values from 0 to 1023, as said below
Outputs:
- density: float32 [2, 64, 4096], P(None, ('row', 'col'))
- moments: float32 [2, 9, 1024], replicated
Inputs may be any that keep to these rules, and one draw needn't show every extreme that they name: `tile_list`: the 7 tile numbers of each batch are 7 consecutive numbers in some order. `tile_count`: some batch has 7. `point_count`: some batch has 4096. `atom_of_point`: the points of batch g belong to atoms (g * 16 + j) mod 1024 with j from 0 to 7.
All inputs are finite; a program needn't handle non-finite values.
Results may differ from a plain program's by a relative error of at most 0.0003.
Values may be sent and summed in bfloat16 or wider, within the bound.
A program may use at most 192 MiB of HBM per device.

v0:
```python
import jax
import jax.numpy as jnp
from jax import lax
from jax.sharding import PartitionSpec as P

TILE = 128
ATOMS = 1024


def harmonics(offsets):
    first_axis = offsets[0]
    second_axis = offsets[1]
    third_axis = offsets[2]
    radius_sq = first_axis * first_axis + second_axis * second_axis + third_axis * third_axis
    return jnp.stack(
        [
            jnp.ones_like(first_axis),
            first_axis,
            second_axis,
            third_axis,
            first_axis * second_axis,
            second_axis * third_axis,
            3.0 * third_axis * third_axis - radius_sq,
            first_axis * third_axis,
            first_axis * first_axis - second_axis * second_axis,
        ]
    )


def local(
    density_first,
    density_second,
    basis,
    tile_list,
    tile_count,
    point_count,
    offsets,
    weights,
    atom_of_point,
):
    row_count = lax.axis_size("row")
    col_count = lax.axis_size("col")
    tile_size = TILE
    local_rows = density_first.shape[0] // tile_size
    local_cols = density_first.shape[1] // tile_size
    batches_dev = tile_list.shape[0]
    run_length = tile_list.shape[1]
    points = basis.shape[1]
    row_slots = -(-run_length // row_count)
    col_slots = -(-run_length // col_count)
    my_row = lax.axis_index("row")
    my_col = lax.axis_index("col")
    own_start = jnp.min(tile_list, axis=1)
    starts = lax.all_gather(own_start, ("row", "col"), axis=0, tiled=True)
    run_end = starts[:, None] + run_length
    first_row = starts + (my_row - starts) % row_count
    row_tile = first_row[:, None] + row_count * jnp.arange(row_slots, dtype=jnp.int32)[None, :]
    row_ok = row_tile < run_end
    row_local = jnp.where(row_ok, row_tile // row_count, 0)
    first_col = starts + (my_col - starts) % col_count
    col_tile = first_col[:, None] + col_count * jnp.arange(col_slots, dtype=jnp.int32)[None, :]
    col_ok = col_tile < run_end
    col_local = jnp.where(col_ok, col_tile // col_count, 0)
    wanted = row_ok[:, :, None] & col_ok[:, None, :]

    def pack_tiles(stored):
        tile_grid = stored.reshape(local_rows, tile_size, local_cols, tile_size).transpose(
            0, 2, 1, 3
        )
        picked = tile_grid[row_local[:, :, None], col_local[:, None, :]]
        picked = jnp.where(wanted[..., None, None], picked, jnp.zeros((), stored.dtype))
        return picked.reshape(
            row_count, col_count, batches_dev, row_slots, col_slots, tile_size, tile_size
        )

    outgoing_first = pack_tiles(density_first)
    outgoing_second = pack_tiles(density_second)
    flat_shape = (row_count * col_count,) + outgoing_first.shape[2:]
    flat_first = outgoing_first.reshape(flat_shape)
    flat_second = outgoing_second.reshape(flat_shape)
    moved_first, moved_second = (
        lax.all_to_all(flat_first, ("row", "col"), split_axis=0, concat_axis=0, tiled=True),
        lax.all_to_all(flat_second, ("row", "col"), split_axis=0, concat_axis=0, tiled=True),
    )
    arrived_first = moved_first.reshape(outgoing_first.shape)
    arrived_second = moved_second.reshape(outgoing_second.shape)
    offset_in_run = tile_list - own_start[:, None]
    owner_row = tile_list % row_count
    slot_row = offset_in_run // row_count
    owner_col = tile_list % col_count
    slot_col = offset_in_run // col_count
    batch_ids = jnp.arange(batches_dev, dtype=jnp.int32)[:, None, None]

    def assemble(arrived):
        blocks = arrived[
            owner_row[:, :, None],
            owner_col[:, None, :],
            batch_ids,
            slot_row[:, :, None],
            slot_col[:, None, :],
        ]
        return blocks.transpose(0, 1, 3, 2, 4).reshape(
            batches_dev, run_length * tile_size, run_length * tile_size
        )

    col_mask = jnp.arange(run_length)[None, :] < tile_count[:, None]
    col_mask = jnp.repeat(col_mask, tile_size, axis=1).astype(jnp.bfloat16)
    masked = basis * col_mask[:, None, :]
    point_mask = (jnp.arange(points)[None, :] < point_count[:, None]).astype(jnp.float32)

    def density_of(arrived):
        block = assemble(arrived)
        product = jnp.einsum("bpi,bij->bpj", masked, block, preferred_element_type=jnp.float32)
        return jnp.sum(product * masked.astype(jnp.float32), axis=2) * point_mask

    density = jnp.stack([density_of(arrived_first), density_of(arrived_second)])
    harmonic = harmonics(offsets)
    moment_terms = density[:, None] * (weights[None, None] * harmonic[None])
    flat_terms = moment_terms.reshape(2 * 9, -1)
    one_hot = (
        atom_of_point.reshape(-1)[:, None] == jnp.arange(ATOMS, dtype=jnp.int32)[None, :]
    ).astype(jnp.float32)
    partial_value = jnp.dot(
        flat_terms, one_hot, precision=lax.Precision.HIGHEST, preferred_element_type=jnp.float32
    )
    moments = lax.psum(partial_value, ("row", "col"))
    return (density, moments.reshape(2, 9, ATOMS))


def solution(mesh):
    placed = (
        P("row", "col"),
        P("row", "col"),
        P(("row", "col"), None, None),
        P(("row", "col"), None),
        P(("row", "col")),
        P(("row", "col")),
        P(None, ("row", "col"), None),
        P(("row", "col"), None),
        P(("row", "col"), None),
    )
    return jax.shard_map(
        local,
        mesh=mesh,
        in_specs=placed,
        out_specs=(P(None, ("row", "col"), None), P()),
        check_vma=False,
    )
```

profile of v0, /device:TPU:0, one launch (start us, length us, event | category | flops | bytes accessed | tf_op | source)
XLA Modules:
  0.0 516.1 jit_solution(7729851914212681637)
XLA Ops:
  7.2 0.8 fusion.11
  8.2 42.0 %all-reduce = s32[64]{0:T(128)S(1)} all-reduce(s32[64]{0:T(128)S(1)} %dynamic-update-slice), channel_id=1, replica_groups=mesh['row'=8,'col'=4] {'row','col'}, use_global_device_ids=true, to_apply=%add | all-reduce | flops 64 | bytes 512
  50.8 9.8 %copy.68 = bf16[192,8,24,128]{3,2,1,0:T(8,128)(2,1)} copy(bf16[192,8,24,128]{3,1,2,0:T(8,128)(2,1)} %bitcast.60) | data formatting | bytes 18874368
  60.6 10.0 %copy.75 = bf16[12,128,24,128]{3,1,2,0:T(8,128)(2,1)} copy(bf16[12,128,24,128]{3,2,1,0:T(8,128)(2,1)} %bitcast.51) | data formatting | bytes 18874368 | tf_op jit(solution)/shard_map/reshape | solution.py:67
  70.6 9.9 %copy.67 = bf16[192,8,24,128]{3,2,1,0:T(8,128)(2,1)} copy(bf16[192,8,24,128]{3,1,2,0:T(8,128)(2,1)} %bitcast.61) | data formatting | bytes 18874368
  80.5 10.1 %copy.76 = bf16[12,128,24,128]{3,1,2,0:T(8,128)(2,1)} copy(bf16[12,128,24,128]{3,2,1,0:T(8,128)(2,1)} %bitcast.52) | data formatting | bytes 18874368 | tf_op jit(solution)/shard_map/reshape | solution.py:67
  90.6 6.8 %gather_fusion.2 = bf16[128,128,128]{2,1,0:T(8,128)(2,1)} fusion(bf16[12,24,128,128]{3,2,1,0:T(8,128)(2,1)} %bitcast.53, s32[128]{0:T(128)S(1)} %reshape.452), kind=kCustom, calls=%fused_computation.2 | custom fusion | bytes 8389632 | tf_op jit(solution)/shard_map/gather | solution.py:70
  97.4 6.7 %gather_fusion = bf16[128,128,128]{2,1,0:T(8,128)(2,1)} fusion(bf16[12,24,128,128]{3,2,1,0:T(8,128)(2,1)} %bitcast.54, s32[128]{0:T(128)S(1)} %reshape.452), kind=kCustom, calls=%fused_computation | custom fusion | bytes 8389632 | tf_op jit(solution)/shard_map/gather | solution.py:70
  104.5 5.2 broadcast_select_fusion.1
  109.6 97.9 %all_to_all.10 = bf16[32,2,1,2,128,128]{5,4,3,1,2,0:T(8,128)(2,1)} all-to-all(bf16[32,2,1,2,128,128]{5,4,3,1,2,0:T(8,128)(2,1)S(1)} %get-tuple-element.13), channel_id=1, replica_groups=mesh['row'=8,'col'=4] {'row','col'}, dimensions={0} | all-to-all | bytes 8388608 | tf_op jit(solution)/shard_map/all_to_all | solution.py:83
  207.5 3.8 all-to-all-start
  212.2 19.9 %copy.46 = bf16[2,4096,896]{1,2,0:T(8,128)(2,1)} copy(bf16[2,4096,896]{2,1,0:T(8,128)(2,1)} %param.11) | data formatting | bytes 29360128 | tf_op args[2]
  232.6 4.2 gather_fusion.3
  236.9 4.5 copy.56
  241.4 7.4 %reshape.487 = bf16[2,896,896]{2,1,0:T(8,128)(2,1)} reshape(bf16[2,7,128,7,128]{4,3,2,1,0:T(8,128)(2,1)} %copy.56) | data formatting | bytes 6422528 | tf_op jit(solution)/shard_map/reshape | solution.py:102
  248.8 56.7 %all-to-all-done = bf16[32,2,1,2,128,128]{5,4,3,1,2,0:T(8,128)(2,1)} async-done(((bf16[32,2,1,2,128,128]{5,4,3,1,2,0:T(8,128)(2,1)}), bf16[32,2,1,2,128,128]{5,4,3,1,2,0:T(8,128)(2,1)}, u32[]{:S(2)}, u32[]{:S(2)}) %all-to-all-start) | async-done | bytes 4194336 | tf_op jit(solution)/shard_map/all_to_all | solution.py:82
  305.6 4.2 gather_fusion.1
  309.8 4.5 copy.51
  314.3 7.6 %reshape.485 = bf16[2,896,896]{2,1,0:T(8,128)(2,1)} reshape(bf16[2,7,128,7,128]{4,3,2,1,0:T(8,128)(2,1)} %copy.51) | data formatting | bytes 6422528 | tf_op jit(solution)/shard_map/reshape | solution.py:102
  321.9 23.4 %fusion.2 = f32[2,4096]{1,0:T(2,128)S(1)} fusion(bf16[2,896,896]{2,1,0:T(8,128)(2,1)S(1)} %copy-done, bf16[2,4096,896]{1,2,0:T(8,128)(2,1)} %copy.46, bf16[2,896]{1,0:T(2,128)(2,1)S(1)} %bitcast.68), kind=kOutput, calls=%fused_computation.9 | convolution fusion | flops 13190029312 | bytes 17927680 | tf_op jit(solution)/shard_map/bpi,bij->bpj/dot_general | solution.py:113
  345.3 24.4 %fusion.1 = f32[2,4096]{1,0:T(2,128)S(1)} fusion(bf16[2,896,896]{2,1,0:T(8,128)(2,1)} %reshape.485, bf16[2,4096,896]{1,2,0:T(8,128)(2,1)} %copy.46, bf16[2,896]{1,0:T(2,128)(2,1)S(1)} %bitcast.69), kind=kOutput, calls=%fused_computation.8 | convolution fusion | flops 13190029312 | bytes 17927680 | tf_op jit(solution)/shard_map/bpi,bij->bpj/dot_general | solution.py:113
  371.0 10.5 %fusion = f32[18,1024]{1,0:T(8,128)S(1)} fusion(f32[18,8192]{1,0:T(8,128)S(1)} %bitcast.64, s32[8192]{0:T(1024)S(1)} %bitcast.66), kind=kOutput, calls=%fused_computation.7 | convolution fusion | flops 1820327936 | bytes 696320 | tf_op jit(solution)/shard_map/dot_general | solution.py:123
  382.2 125.1 %all-reduce.3.cloned.1.call-done = f32[2,9,1024]{2,1,0:T(8,128)} async-done(((f32[2,9,1024]{2,1,0:T(8,128)}), f32[2,9,1024]{2,1,0:T(8,128)}) %all-reduce.3.cloned.1.call-update) | async-done | bytes 73744 | tf_op jit(solution)/shard_map/psum | solution.py:126
  507.3 1.6 copy.59
  (55 shorter events, 4.2 us)
Async XLA Ops:
  207.5 4.3 copy-start.5
  207.5 98.0 %all-to-all-start = ((bf16[32,2,1,2,128,128]{5,4,3,1,2,0:T(8,128)(2,1)}), bf16[32,2,1,2,128,128]{5,4,3,1,2,0:T(8,128)(2,1)}, u32[]{:S(2)}, u32[]{:S(2)}) async-start(bf16[32,2,1,2,128,128]{5,4,3,1,2,0:T(8,128)(2,1)} %get-tuple-element.12), calls=%async_computation | async-start | bytes 8388608 | tf_op jit(solution)/shard_map/all_to_all | solution.py:82
  211.3 295.9 %all-reduce.3.cloned.1.call-start = ((), (), s32[]{:S(2)}) async-start(), calls=%async_computation.2 | async-start | bytes 262144 | tf_op jit(solution)/shard_map/psum | solution.py:126
  212.1 20.0 %copy-start.7 = (s32[2]{0:T(128)S(1)}, s32[2]{0:T(128)}, u32[]{:S(2)}) copy-start(s32[2]{0:T(128)} %param.13) | copy-start | bytes 28
  212.1 20.1 %copy-start.4 = (s32[2,4096]{1,0:T(2,128)S(1)}, s32[2,4096]{1,0:T(2,128)}, u32[]{:S(2)}) copy-start(s32[2,4096]{1,0:T(2,128)} %param.17) | copy-start | bytes 98308
  212.1 20.1 %copy-start.1 = (f32[3,2,4096]{2,1,0:T(2,128)S(1)}, f32[3,2,4096]{2,1,0:T(2,128)}, u32[]{:S(2)}) copy-start(f32[3,2,4096]{2,1,0:T(2,128)} %param.15) | copy-start | bytes 294916
  212.2 20.3 %copy-start.3 = (f32[2,4096]{1,0:T(2,128)S(1)}, f32[2,4096]{1,0:T(2,128)}, u32[]{:S(2)}) copy-start(f32[2,4096]{1,0:T(2,128)} %param.16) | copy-start | bytes 98308
  314.3 7.6 %copy-start = (bf16[2,896,896]{2,1,0:T(8,128)(2,1)S(1)}, bf16[2,896,896]{2,1,0:T(8,128)(2,1)}, u32[]{:S(2)}) copy-start(bf16[2,896,896]{2,1,0:T(8,128)(2,1)} %reshape.487) | copy-start | bytes 9633796
  345.3 24.5 %copy-start.6 = (s32[2]{0:T(128)S(1)}, s32[2]{0:T(128)}, u32[]{:S(2)}) copy-start(s32[2]{0:T(128)} %param.14) | copy-start | bytes 28
  369.9 11.6 %copy-start.2 = (f32[2,2,4096]{2,1,0:T(2,128)}, f32[2,2,4096]{2,1,0:T(2,128)S(1)}, u32[]{:S(2)}) copy-start(f32[2,2,4096]{2,1,0:T(2,128)S(1)} %pad_maximum_fusion) | copy-start | bytes 196612
Sparse Core Ops, SparseCore 0:
  382.3 124.9 all-reduce.2
where the time goes:
time: 525 us; the launch traced here: 516 us
  waiting for transfers between devices  182 us (35%)
  blocking collectives  140 us (27%)
  local copies, waits for them, and re-layouts  110 us (21%)
  matrix products  58.4 us (11%)
  between operations  14.7 us (3%)
  other arithmetic  7.15 us (1%)
    psum x1, waiting for transfers between devices, local(): moments = lax.psum(partial_value, ('row', 'col'))  125 us
    all_to_all x1, blocking collectives, local(): lax.all_to_all(flat_second, ('row', 'col'), split_axis=0, concat_axis=0,...  97.9 us
    all_to_all x1, waiting for transfers between devices, local(): lax.all_to_all(flat_first, ('row', 'col'), split_axis=0, concat_axis=0, t...  56.7 us
    dot_general x2, matrix products, density_of(): jnp.einsum('bpi,bij->bpj', masked, block, preferred_element_type=jnp.floa...  47.8 us
    unnamed x29, local copies, waits for them, and re-layouts  42.4 us
    unnamed x1, blocking collectives  42 us
    reshape x2, local copies, waits for them, and re-layouts, pack_tiles(): stored.reshape(local_rows, tile_size, local_cols, tile_size)  20.1 us
    reshape x2, local copies, waits for them, and re-layouts, assemble(): blocks.transpose(0, 1, 3, 2, 4)  15 us
  transfers between devices with their start and end apart: 2, of which 2 were waited for; matrix products, arithmetic and copies ran while one was open for 7% of the time, Pallas kernels for 0%

commit v1 on v0

--- a/solution.py
+++ b/solution.py
@@ -123,7 +123,7 @@
     partial_value = jnp.dot(
         flat_terms, one_hot, precision=lax.Precision.HIGHEST, preferred_element_type=jnp.float32
     )
-    moments = lax.psum(partial_value, ("row", "col"))
+    moments = jnp.sum(lax.all_gather(partial_value, ("row", "col")), axis=0)
     return (density, moments.reshape(2, 9, ATOMS))
 
 

time: 525 us -> 461 us (0.88)
  waiting for transfers between devices: 182 us -> 117 us
    psum x1 -> x0, waiting for transfers between devices: 125 us -> none  [local(): moments = lax.psum(partial_value, ('row', 'col'))]
    all_gather x0 -> x1, waiting for transfers between devices: none -> 59.8 us  [local(): moments = jnp.sum(lax.all_gather(partial_value, ('row', 'col')), axis=0)]
  transfers between devices with their start and end apart: 2 -> 2, of which waited for: 2 -> 2; matrix products, arithmetic and copies ran while one was open for 7% -> 8% of each run, Pallas kernels for 0% -> 0%
where the time goes in v1:
time: 461 us; the launch traced here: 452 us
  blocking collectives  140 us (30%)
  waiting for transfers between devices  117 us (25%)
  local copies, waits for them, and re-layouts  108 us (23%)
  matrix products  59 us (13%)
  between operations  14.7 us (3%)
  other arithmetic  9.25 us (2%)
    all_to_all x1, blocking collectives, local(): lax.all_to_all(flat_second, ('row', 'col'), split_axis=0, concat_axis=0,...  97.9 us
    all_gather x1, waiting for transfers between devices, local(): moments = jnp.sum(lax.all_gather(partial_value, ('row', 'col')), axis=0)  59.8 us
    all_to_all x1, waiting for transfers between devices, local(): lax.all_to_all(flat_first, ('row', 'col'), split_axis=0, concat_axis=0, t...  56.7 us
    dot_general x2, matrix products, density_of(): jnp.einsum('bpi,bij->bpj', masked, block, preferred_element_type=jnp.floa...  47.8 us
    unnamed x1, blocking collectives  42 us
    unnamed x29, local copies, waits for them, and re-layouts  41.5 us
    reshape x2, local copies, waits for them, and re-layouts, pack_tiles(): stored.reshape(local_rows, tile_size, local_cols, tile_size)  20.1 us
    reshape x2, local copies, waits for them, and re-layouts, assemble(): blocks.transpose(0, 1, 3, 2, 4)  15 us
  transfers between devices with their start and end apart: 2, of which 2 were waited for; matrix products, arithmetic and copies ran while one was open for 8% of the time, Pallas kernels for 0%

profile of v1, /device:TPU:0, one launch (start us, length us, event | category | flops | bytes accessed | tf_op | source)
XLA Modules:
  0.0 452.0 jit_solution(12406237800808099856)
XLA Ops:
  7.2 0.8 fusion.12
  8.2 42.0 %all-reduce = s32[64]{0:T(128)S(1)} all-reduce(s32[64]{0:T(128)S(1)} %dynamic-update-slice), channel_id=1, replica_groups=mesh['row'=8,'col'=4] {'row','col'}, use_global_device_ids=true, to_apply=%add | all-reduce | flops 64 | bytes 512
  50.8 9.8 %copy.67 = bf16[192,8,24,128]{3,2,1,0:T(8,128)(2,1)} copy(bf16[192,8,24,128]{3,1,2,0:T(8,128)(2,1)} %bitcast.62) | data formatting | bytes 18874368
  60.6 10.0 %copy.74 = bf16[12,128,24,128]{3,1,2,0:T(8,128)(2,1)} copy(bf16[12,128,24,128]{3,2,1,0:T(8,128)(2,1)} %bitcast.53) | data formatting | bytes 18874368 | tf_op jit(solution)/shard_map/reshape | solution.py:67
  70.6 9.9 %copy.66 = bf16[192,8,24,128]{3,2,1,0:T(8,128)(2,1)} copy(bf16[192,8,24,128]{3,1,2,0:T(8,128)(2,1)} %bitcast.63) | data formatting | bytes 18874368
  80.5 10.1 %copy.75 = bf16[12,128,24,128]{3,1,2,0:T(8,128)(2,1)} copy(bf16[12,128,24,128]{3,2,1,0:T(8,128)(2,1)} %bitcast.54) | data formatting | bytes 18874368 | tf_op jit(solution)/shard_map/reshape | solution.py:67
  90.6 6.8 %gather_fusion.2 = bf16[128,128,128]{2,1,0:T(8,128)(2,1)} fusion(bf16[12,24,128,128]{3,2,1,0:T(8,128)(2,1)} %bitcast.55, s32[128]{0:T(128)S(1)} %reshape.452), kind=kCustom, calls=%fused_computation.2 | custom fusion | bytes 8389632 | tf_op jit(solution)/shard_map/gather | solution.py:70
  97.4 6.7 %gather_fusion = bf16[128,128,128]{2,1,0:T(8,128)(2,1)} fusion(bf16[12,24,128,128]{3,2,1,0:T(8,128)(2,1)} %bitcast.56, s32[128]{0:T(128)S(1)} %reshape.452), kind=kCustom, calls=%fused_computation | custom fusion | bytes 8389632 | tf_op jit(solution)/shard_map/gather | solution.py:70
  104.5 5.2 %broadcast_select_fusion.1 = (bf16[32,2,1,2,128,128]{5,4,3,1,2,0:T(8,128)(2,1)}, bf16[32,2,1,2,128,128]{5,4,3,1,2,0:T(8,128)(2,1)S(1)}) fusion(bf16[32,2,1,2,128,128]{5,4,3,1,2,0:T(8,128)(2,1)} %bitcast.58, pred[32,2,2]{2,1,0:T(4,128)(4,1)S(1)} %compare_and_fusion, bf16[32,2,1,2,128,128]{5,4,3,1,2,0:T(8,128)(2,1)} %bitcast.57), kind=kLoop, calls=%fused_computation.18 | loop fusion | flops 4194304 | bytes 16777344 | tf_op jit(solution)/shard_map/jit(_where)/select_n | solution.py:71
  109.6 97.9 %all_to_all.10 = bf16[32,2,1,2,128,128]{5,4,3,1,2,0:T(8,128)(2,1)} all-to-all(bf16[32,2,1,2,128,128]{5,4,3,1,2,0:T(8,128)(2,1)S(1)} %get-tuple-element.13), channel_id=1, replica_groups=mesh['row'=8,'col'=4] {'row','col'}, dimensions={0} | all-to-all | bytes 8388608 | tf_op jit(solution)/shard_map/all_to_all | solution.py:83
  207.5 3.8 all-to-all-start
  212.2 19.9 %copy.45 = bf16[2,4096,896]{1,2,0:T(8,128)(2,1)} copy(bf16[2,4096,896]{2,1,0:T(8,128)(2,1)} %param.11) | data formatting | bytes 29360128 | tf_op args[2]
  232.6 4.2 gather_fusion.3
  236.9 4.5 %copy.55 = bf16[2,7,128,7,128]{4,3,2,1,0:T(8,128)(2,1)} copy(bf16[2,7,128,7,128]{4,2,3,1,0:T(8,128)(2,1)S(1)} %bitcast.61) | data formatting | bytes 6422528 | tf_op jit(solution)/shard_map/transpose | solution.py:102
  241.4 7.4 %reshape.491 = bf16[2,896,896]{2,1,0:T(8,128)(2,1)} reshape(bf16[2,7,128,7,128]{4,3,2,1,0:T(8,128)(2,1)} %copy.55) | data formatting | bytes 6422528 | tf_op jit(solution)/shard_map/reshape | solution.py:102
  248.8 56.7 %all-to-all-done = bf16[32,2,1,2,128,128]{5,4,3,1,2,0:T(8,128)(2,1)} async-done(((bf16[32,2,1,2,128,128]{5,4,3,1,2,0:T(8,128)(2,1)}), bf16[32,2,1,2,128,128]{5,4,3,1,2,0:T(8,128)(2,1)}, u32[]{:S(2)}, u32[]{:S(2)}) %all-to-all-start) | async-done | bytes 4194336 | tf_op jit(solution)/shard_map/all_to_all | solution.py:82
  305.6 4.2 gather_fusion.1
  309.8 4.5 copy.50
  314.3 7.6 %reshape.489 = bf16[2,896,896]{2,1,0:T(8,128)(2,1)} reshape(bf16[2,7,128,7,128]{4,3,2,1,0:T(8,128)(2,1)} %copy.50) | data formatting | bytes 6422528 | tf_op jit(solution)/shard_map/reshape | solution.py:102
  321.9 23.4 %fusion.2 = f32[2,4096]{1,0:T(2,128)S(1)} fusion(bf16[2,896,896]{2,1,0:T(8,128)(2,1)S(1)} %copy-done, bf16[2,4096,896]{1,2,0:T(8,128)(2,1)} %copy.45, bf16[2,896]{1,0:T(2,128)(2,1)S(1)} %bitcast.70), kind=kOutput, calls=%fused_computation.9 | convolution fusion | flops 13190029312 | bytes 17927680 | tf_op jit(solution)/shard_map/bpi,bij->bpj/dot_general | solution.py:113
  345.3 24.4 %fusion.1 = f32[2,4096]{1,0:T(2,128)S(1)} fusion(bf16[2,896,896]{2,1,0:T(8,128)(2,1)} %reshape.489, bf16[2,4096,896]{1,2,0:T(8,128)(2,1)} %copy.45, bf16[2,896]{1,0:T(2,128)(2,1)S(1)} %bitcast.71), kind=kOutput, calls=%fused_computation.8 | convolution fusion | flops 13190029312 | bytes 17927680 | tf_op jit(solution)/shard_map/bpi,bij->bpj/dot_general | solution.py:113
  371.0 11.2 %fusion.8 = f32[1,18,1024]{2,1,0:T(8,128)} fusion(f32[18,8192]{1,0:T(8,128)S(1)} %bitcast.66, s32[8192]{0:T(1024)S(1)} %bitcast.68), kind=kOutput, calls=%fused_computation.19 | convolution fusion | flops 1820327936 | bytes 696320 | tf_op jit(solution)/shard_map/dot_general | solution.py:123
  382.2 59.8 %all-gather.4.cloned.1.call-done = f32[32,18,1024]{2,1,0:T(8,128)} async-done(((f32[1,18,1024]{2,1,0:T(8,128)}), f32[32,18,1024]{2,1,0:T(8,128)}) %all-gather.4.cloned.1.call-update) | async-done | bytes 2359312 | tf_op jit(solution)/shard_map/all_gather | solution.py:126
  441.9 2.1 reduce_sum.35
  (56 shorter events, 4.3 us)
Async XLA Ops:
  207.5 4.3 copy-start.5
  207.5 98.0 %all-to-all-start = ((bf16[32,2,1,2,128,128]{5,4,3,1,2,0:T(8,128)(2,1)}), bf16[32,2,1,2,128,128]{5,4,3,1,2,0:T(8,128)(2,1)}, u32[]{:S(2)}, u32[]{:S(2)}) async-start(bf16[32,2,1,2,128,128]{5,4,3,1,2,0:T(8,128)(2,1)} %get-tuple-element.12), calls=%async_computation | async-start | bytes 8388608 | tf_op jit(solution)/shard_map/all_to_all | solution.py:82
  211.3 230.6 %all-gather.4.cloned.1.call-start = ((), (), s32[]{:S(2)}) async-start(), calls=%async_computation.2 | async-start | bytes 3244032 | tf_op jit(solution)/shard_map/all_gather | solution.py:126
  212.1 20.0 %copy-start.7 = (s32[2]{0:T(128)S(1)}, s32[2]{0:T(128)}, u32[]{:S(2)}) copy-start(s32[2]{0:T(128)} %param.13) | copy-start | bytes 28
  212.1 20.1 %copy-start.4 = (s32[2,4096]{1,0:T(2,128)S(1)}, s32[2,4096]{1,0:T(2,128)}, u32[]{:S(2)}) copy-start(s32[2,4096]{1,0:T(2,128)} %param.17) | copy-start | bytes 98308
  212.1 20.1 %copy-start.1 = (f32[3,2,4096]{2,1,0:T(2,128)S(1)}, f32[3,2,4096]{2,1,0:T(2,128)}, u32[]{:S(2)}) copy-start(f32[3,2,4096]{2,1,0:T(2,128)} %param.15) | copy-start | bytes 294916
  212.2 20.3 %copy-start.3 = (f32[2,4096]{1,0:T(2,128)S(1)}, f32[2,4096]{1,0:T(2,128)}, u32[]{:S(2)}) copy-start(f32[2,4096]{1,0:T(2,128)} %param.16) | copy-start | bytes 98308
  314.3 7.6 %copy-start = (bf16[2,896,896]{2,1,0:T(8,128)(2,1)S(1)}, bf16[2,896,896]{2,1,0:T(8,128)(2,1)}, u32[]{:S(2)}) copy-start(bf16[2,896,896]{2,1,0:T(8,128)(2,1)} %reshape.491) | copy-start | bytes 9633796
  345.3 24.5 %copy-start.6 = (s32[2]{0:T(128)S(1)}, s32[2]{0:T(128)}, u32[]{:S(2)}) copy-start(s32[2]{0:T(128)} %param.14) | copy-start | bytes 28
  369.9 12.3 %copy-start.2 = (f32[2,2,4096]{2,1,0:T(2,128)}, f32[2,2,4096]{2,1,0:T(2,128)S(1)}, u32[]{:S(2)}) copy-start(f32[2,2,4096]{2,1,0:T(2,128)S(1)} %pad_maximum_fusion) | copy-start | bytes 196612
Sparse Core Ops, SparseCore 0:
  382.3 59.5 all-gather.3
